TPU v7x, 32 devices: a whole 2x2x4 slice. The times are simulated.
32 devices in a mesh: row: 4 (over y, x), col: 4 (over z), depth: 2 (over core).
Axes of the slice: x: 2, y: 2, z: 4, core: 2. Of those that a mesh axis runs over, the one named last changes fastest.
Arguments:
- halves: bfloat16 [2, 8192, 16384], P(None, 'row', ('col', 'depth')), may hold values from -6 to 6
- spectrum: float32 [2, 16384], P(None, ('col', 'depth')), as said below
- wanted: int32 [4096], P('col'), may hold values from 0 to 32766, as said below
- fraction: float32 [4096], P('col'), may hold values from 0.05 to 0.95
Outputs:
- eigvec: float32 [2, 8192, 4096], P(None, 'row', ('col', 'depth'))
Inputs may be any that keep to these rules, and one draw needn't show every extreme that they name: Read in the order spectrum[0,0], spectrum[1,0], spectrum[0,1], spectrum[1,1], ... the values rise strictly, each by more than 0.05 over the one before. `wanted`: distinct positions in that merged order of the 32768 eigenvalues.
All inputs are finite; a program needn't handle non-finite values.
Results may differ from a plain program's by a relative error of at most 0.0029.
Values may be sent and summed in bfloat16 or wider, within the bound.
A program may use at most 192 MiB of HBM per device.

v0:
```python
import math
import jax
import jax.numpy as jnp
from jax import lax
from jax.sharding import PartitionSpec as P


def broadcast(shard, axis, root):
    mine = lax.axis_index(axis) == root
    return lax.psum(jnp.where(mine, shard, jnp.zeros_like(shard)), axis)


def root_terms(spectrum_full, wanted):
    ordered = jnp.stack([spectrum_full[0], spectrum_full[1]], axis=1).reshape(-1)
    lower = jnp.take(ordered, wanted)
    upper = jnp.take(ordered, wanted + 1)
    return (lower, upper - lower)


def cauchy_block(seam_part, value_part, lower, width, frac):
    return seam_part[:, :, None] / (
        value_part[:, :, None] - lower[None, None, :] - frac[None, None, :] * width[None, None, :]
    )


def column_norms(seam_full, value_full, lower, width, frac):
    step = seam_full.shape[1] // 8
    total = jnp.zeros(lower.shape, jnp.float32)
    for part in range(8):
        cauchy = cauchy_block(
            seam_full[:, part * step : (part + 1) * step],
            value_full[:, part * step : (part + 1) * step],
            lower,
            width,
            frac,
        )
        total = total + jnp.sum(cauchy * cauchy, axis=(0, 1))
    return jnp.sqrt(total)


def panel_product(piece, seam_part, value_part, lower, width, frac):
    columns = lower.shape[0]
    block = math.gcd(columns, 128)

    def one(index):
        start = index * block
        low = lax.dynamic_slice_in_dim(lower, start, block)
        wid = lax.dynamic_slice_in_dim(width, start, block)
        frc = lax.dynamic_slice_in_dim(frac, start, block)
        cauchy = cauchy_block(seam_part, value_part, low, wid, frc)
        product = jnp.einsum(
            "arh,ahk->ark", piece, cauchy.astype(jnp.bfloat16), preferred_element_type=jnp.float32
        )
        return (product, jnp.zeros((block,), jnp.float32))

    products, sums = lax.map(one, jnp.arange(columns // block))
    product = jnp.transpose(products, (1, 2, 0, 3)).reshape(piece.shape[0], piece.shape[1], columns)
    return (product, sums.reshape(-1))


def body(halves, spectrum, wanted, fraction):
    rows_here = halves.shape[1]
    shard_width = halves.shape[2]
    last = broadcast(halves[0, rows_here - 1], "row", lax.axis_size("row") - 1)
    first = broadcast(halves[1, 0], "row", 0)
    seam = jnp.stack([last, first]).astype(jnp.float32)
    seam_full, value_full = (
        lax.all_gather(seam, ("col", "depth"), axis=1, tiled=True),
        lax.all_gather(spectrum, ("col", "depth"), axis=1, tiled=True),
    )
    lower_col, width_col = root_terms(value_full, wanted)
    ncols = lax.axis_size("col")
    ndepth = lax.axis_size("depth")
    layer = lax.axis_index("depth")
    seam_mine = lax.dynamic_index_in_dim(
        seam_full.reshape(2, ncols, ndepth, shard_width), layer, 2, keepdims=False
    ).reshape(2, ncols * shard_width)
    value_mine = lax.dynamic_index_in_dim(
        value_full.reshape(2, ncols, ndepth, shard_width), layer, 2, keepdims=False
    ).reshape(2, ncols * shard_width)
    share = lower_col.shape[0] // ndepth
    product, sums = panel_product(
        lax.all_gather(halves, "col", axis=2, tiled=True),
        seam_mine,
        value_mine,
        lower_col,
        width_col,
        fraction,
    )
    total = product
    product = lax.psum_scatter(total, "depth", scatter_dimension=2, tiled=True)
    lower_own = lax.dynamic_slice_in_dim(lower_col, layer * share, share)
    width_own = lax.dynamic_slice_in_dim(width_col, layer * share, share)
    frac_own = lax.dynamic_slice_in_dim(fraction, layer * share, share)
    norms = column_norms(seam_full, value_full, lower_own, width_own, frac_own)
    return product / norms[None, None, :]


def solution(mesh):
    in_specs = (P(None, "row", ("col", "depth")), P(None, ("col", "depth")), P("col"), P("col"))
    out_specs = P(None, "row", ("col", "depth"))
    return jax.shard_map(body, mesh=mesh, in_specs=in_specs, out_specs=out_specs, check_vma=False)
```

profile of v0, /device:TPU:0, one launch (start us, length us, event | category | flops | bytes accessed | tf_op | source)
XLA Modules:
  0.0 1443.4 jit_solution(10954515901074154995)
XLA Ops:
  6.5 0.7 all-gather.2.cloned.1.call-update
  7.3 15.7 %all_gather.10 = f32[2,16384]{1,0:T(2,128)S(1)} all-gather(f32[2,2048]{1,0:T(2,128)S(1)} %copy-done.4), channel_id=1, replica_groups=mesh['row'=4,'col'=4,'depth'=2] {'col','depth'}, dimensions={1}, use_global_device_ids=true | all-gather | bytes 147456 | tf_op jit(solution)/shard_map/all_gather | solution.py:69
  23.7 7.2 copy.11
  30.9 8.2 reshape.75
  39.2 6.2 gather_fusion
  45.3 6.2 gather_fusion.1
  51.5 0.8 fusion.7
  52.3 16.1 %all-reduce = (bf16[1,2048]{1,0:T(2,128)(2,1)S(1)}, bf16[1,2048]{1,0:T(2,128)(2,1)S(1)}) all-reduce(bf16[1,2048]{1,0:T(2,128)(2,1)S(1)} %get-tuple-element.83, bf16[1,2048]{1,0:T(2,128)(2,1)S(1)} %get-tuple-element.82), channel_id=1, replica_groups=mesh['row'=4,'col'=4,'depth'=2] {'row'}, use_global_device_ids=true, to_apply=%region_1.0 | all-reduce | flops 4096 | bytes 16384 | tf_op jit(solution)/shard_map/psum | solution.py:10
  68.5 68.2 %all_gather.9 = f32[2,16384]{1,0:T(2,128)S(1)} all-gather(f32[2,2048]{1,0:T(2,128)S(1)} %maximum_convert_fusion), channel_id=1, replica_groups=mesh['row'=4,'col'=4,'depth'=2] {'col','depth'}, dimensions={1}, use_global_device_ids=true | all-gather | bytes 147456 | tf_op jit(solution)/shard_map/all_gather | solution.py:68
  137.5 985.8 %all-gather.2.cloned.1.call-done = bf16[2,2048,8192]{2,1,0:T(8,128)(2,1)} async-done(((bf16[2,2048,2048]{2,1,0:T(8,128)(2,1)}), bf16[2,2048,8192]{2,1,0:T(8,128)(2,1)}) %all-gather.2.cloned.1.call-update) | async-done | bytes 67108880 | tf_op jit(solution)/shard_map/all_gather | solution.py:83
  1123.3 245.9 %while.10 = (s32[]{:T(128)}, f32[8,2,2048,128]{2,3,1,0:T(8,128)}, f32[2,4,2048]{2,1,0:T(4,128)S(1)}, f32[2,4,2048]{2,1,0:T(4,128)S(1)}, s32[8]{0:T(128)S(1)}, /*...) while((s32[]{:T(128)}, f32[8,2,2048,128]{2,3,1,0:T(8,128)}, ...), condition=%wide.region_3.5_spmd, body=%wide.region_2.4_spmd.sunk | while | flops 8598323200 | bytes 69603520 | solution.py:56
  1123.3 0.6 dynamic_slice.46
  1124.7 29.3 %fusion.17 = f32[8,2,2048,128]{2,3,1,0:T(8,128)} fusion(f32[8,2,2048,128]{2,3,1,0:T(8,128)} %get-tuple-element.175, s32[]{:T(128)} %get-tuple-element.174, bf16[2,2048,8192]{2,1,0:T(8,128)(2,1)} %get-tuple-element.195, f32[128]{0:T(128)S(1)} %dynamic-slice_multiply_fusion.3, f32[128]{0:T(128)S(1)} %dynamic_slice.47, f32[2,8192]{1,0:T(2,128)S(1)} %bitcast.48, ...), kind=kOutput, calls=%fused_computation.9.clone.1 | convolution fusion | flops 8598323200 | bytes 69338624 | tf_op jit(solution)/shard_map/while/body/eval_jaxpr/arh,ahk->ark/dot_general | solution.py:51
  1154.0 0.6 dynamic_slice.46
  1155.4 29.3 %fusion.17 = f32[8,2,2048,128]{2,3,1,0:T(8,128)} fusion(f32[8,2,2048,128]{2,3,1,0:T(8,128)} %get-tuple-element.175, s32[]{:T(128)} %get-tuple-element.174, bf16[2,2048,8192]{2,1,0:T(8,128)(2,1)} %get-tuple-element.195, f32[128]{0:T(128)S(1)} %dynamic-slice_multiply_fusion.3, f32[128]{0:T(128)S(1)} %dynamic_slice.47, f32[2,8192]{1,0:T(2,128)S(1)} %bitcast.48, ...), kind=kOutput, calls=%fused_computation.9.clone.1 | convolution fusion | flops 8598323200 | bytes 69338624 | tf_op jit(solution)/shard_map/while/body/eval_jaxpr/arh,ahk->ark/dot_general | solution.py:51
  1184.8 0.6 dynamic_slice.46
  1186.2 29.3 %fusion.17 = f32[8,2,2048,128]{2,3,1,0:T(8,128)} fusion(f32[8,2,2048,128]{2,3,1,0:T(8,128)} %get-tuple-element.175, s32[]{:T(128)} %get-tuple-element.174, bf16[2,2048,8192]{2,1,0:T(8,128)(2,1)} %get-tuple-element.195, f32[128]{0:T(128)S(1)} %dynamic-slice_multiply_fusion.3, f32[128]{0:T(128)S(1)} %dynamic_slice.47, f32[2,8192]{1,0:T(2,128)S(1)} %bitcast.48, ...), kind=kOutput, calls=%fused_computation.9.clone.1 | convolution fusion | flops 8598323200 | bytes 69338624 | tf_op jit(solution)/shard_map/while/body/eval_jaxpr/arh,ahk->ark/dot_general | solution.py:51
  1215.5 0.6 dynamic_slice.46
  1216.9 29.3 %fusion.17 = f32[8,2,2048,128]{2,3,1,0:T(8,128)} fusion(f32[8,2,2048,128]{2,3,1,0:T(8,128)} %get-tuple-element.175, s32[]{:T(128)} %get-tuple-element.174, bf16[2,2048,8192]{2,1,0:T(8,128)(2,1)} %get-tuple-element.195, f32[128]{0:T(128)S(1)} %dynamic-slice_multiply_fusion.3, f32[128]{0:T(128)S(1)} %dynamic_slice.47, f32[2,8192]{1,0:T(2,128)S(1)} %bitcast.48, ...), kind=kOutput, calls=%fused_computation.9.clone.1 | convolution fusion | flops 8598323200 | bytes 69338624 | tf_op jit(solution)/shard_map/while/body/eval_jaxpr/arh,ahk->ark/dot_general | solution.py:51
  1246.2 0.6 dynamic_slice.46
  1247.6 29.3 %fusion.17 = f32[8,2,2048,128]{2,3,1,0:T(8,128)} fusion(f32[8,2,2048,128]{2,3,1,0:T(8,128)} %get-tuple-element.175, s32[]{:T(128)} %get-tuple-element.174, bf16[2,2048,8192]{2,1,0:T(8,128)(2,1)} %get-tuple-element.195, f32[128]{0:T(128)S(1)} %dynamic-slice_multiply_fusion.3, f32[128]{0:T(128)S(1)} %dynamic_slice.47, f32[2,8192]{1,0:T(2,128)S(1)} %bitcast.48, ...), kind=kOutput, calls=%fused_computation.9.clone.1 | convolution fusion | flops 8598323200 | bytes 69338624 | tf_op jit(solution)/shard_map/while/body/eval_jaxpr/arh,ahk->ark/dot_general | solution.py:51
  1277.0 0.6 dynamic_slice.46
  1278.4 29.3 %fusion.17 = f32[8,2,2048,128]{2,3,1,0:T(8,128)} fusion(f32[8,2,2048,128]{2,3,1,0:T(8,128)} %get-tuple-element.175, s32[]{:T(128)} %get-tuple-element.174, bf16[2,2048,8192]{2,1,0:T(8,128)(2,1)} %get-tuple-element.195, f32[128]{0:T(128)S(1)} %dynamic-slice_multiply_fusion.3, f32[128]{0:T(128)S(1)} %dynamic_slice.47, f32[2,8192]{1,0:T(2,128)S(1)} %bitcast.48, ...), kind=kOutput, calls=%fused_computation.9.clone.1 | convolution fusion | flops 8598323200 | bytes 69338624 | tf_op jit(solution)/shard_map/while/body/eval_jaxpr/arh,ahk->ark/dot_general | solution.py:51
  1307.7 0.6 dynamic_slice.46
  1309.1 29.4 %fusion.17 = f32[8,2,2048,128]{2,3,1,0:T(8,128)} fusion(f32[8,2,2048,128]{2,3,1,0:T(8,128)} %get-tuple-element.175, s32[]{:T(128)} %get-tuple-element.174, bf16[2,2048,8192]{2,1,0:T(8,128)(2,1)} %get-tuple-element.195, f32[128]{0:T(128)S(1)} %dynamic-slice_multiply_fusion.3, f32[128]{0:T(128)S(1)} %dynamic_slice.47, f32[2,8192]{1,0:T(2,128)S(1)} %bitcast.48, ...), kind=kOutput, calls=%fused_computation.9.clone.1 | convolution fusion | flops 8598323200 | bytes 69338624 | tf_op jit(solution)/shard_map/while/body/eval_jaxpr/arh,ahk->ark/dot_general | solution.py:51
  1339.9 29.3 %fusion.17 = f32[8,2,2048,128]{2,3,1,0:T(8,128)} fusion(f32[8,2,2048,128]{2,3,1,0:T(8,128)} %get-tuple-element.175, s32[]{:T(128)} %get-tuple-element.174, bf16[2,2048,8192]{2,1,0:T(8,128)(2,1)} %get-tuple-element.195, f32[128]{0:T(128)S(1)} %dynamic-slice_multiply_fusion.3, f32[128]{0:T(128)S(1)} %dynamic_slice.47, f32[2,8192]{1,0:T(2,128)S(1)} %bitcast.48, ...), kind=kOutput, calls=%fused_computation.9.clone.1 | convolution fusion | flops 8598323200 | bytes 69338624 | tf_op jit(solution)/shard_map/while/body/eval_jaxpr/arh,ahk->ark/dot_general | solution.py:51
  1369.2 18.1 %copy.12 = f32[2,2048,8,128]{3,2,1,0:T(8,128)} copy(f32[2,2048,8,128]{1,3,0,2:T(8,128)} %bitcast.43) | data formatting | bytes 33554432 | tf_op jit(solution)/shard_map/transpose | solution.py:57
  1387.3 18.0 %reshape.76 = f32[2,2048,1024]{2,1,0:T(8,128)} reshape(f32[2,2048,8,128]{3,2,1,0:T(8,128)} %copy.12) | data formatting | bytes 33554432 | tf_op jit(solution)/shard_map/reshape | solution.py:57
  1405.5 0.7 copy-done.3
  1406.3 16.1 %multiply_reduce_fusion.6 = (f32[512]{0:T(512)S(1)}, f32[512]{0:T(512)S(1)}, f32[512]{0:T(512)S(1)}, f32[512]{0:T(512)S(1)}, f32[512]{0:T(512)S(1)}, /*index=5*/f32[512]{0:T(512)S(1)}, f32[512]{0:T(512)S(1)}, f32[512]{0:T(512)S(1)}) fusion(f32[2,2048]{1,0:T(2,128)S(1)} %get-tuple-element.99, f32[2,2048]{1,0:T(2,128)S(1)} %get-tuple-element.91, ...), kind=kLoop, calls=%fused_computation.17 | loop fusion | flops 83881984 | bytes 282624 | tf_op jit(solution)/shard_map/reduce_sum | solution.py:37
  1422.5 6.2 reduce-scatter.2.cloned.1.call-done
  1428.7 7.9 broadcast_divide_fusion
  (67 shorter events, 4.4 us)
Async XLA Ops:
  6.5 0.8 copy-start.4
  6.5 1116.7 %all-gather.2.cloned.1.call-start = ((), (), s32[]{:S(2)}) async-start(), calls=%async_computation.1 | async-start | bytes 83886080 | tf_op jit(solution)/shard_map/all_gather | solution.py:83
  7.3 1421.4 %reduce-scatter.2.cloned.1.call-start = ((), (), s32[]{:S(2)}) async-start(), calls=%async_computation.2 | async-start | bytes 25165824 | tf_op jit(solution)/shard_map/reduce_scatter | solution.py:91
  23.1 0.6 copy-start
  23.7 15.4 %copy-start.5 = (s32[1024]{0:T(1024)S(1)}, s32[1024]{0:T(1024)}, u32[]{:S(2)}) copy-start(s32[1024]{0:T(1024)} %param.10) | copy-start | bytes 12292
  30.9 1092.4 %copy-start.6 = (f32[1024]{0:T(1024)S(1)}, f32[1024]{0:T(1024)}, u32[]{:S(2)}) copy-start(f32[1024]{0:T(1024)} %param.11) | copy-start | bytes 12292
  136.6 0.7 copy-start.2
  1405.3 0.9 copy-start.3
  1405.4 1.0 copy-start.1
Sparse Core Ops, SparseCore 0:
  8.9 1114.3 all-gather.1
  1405.5 23.1 reduce-scatter.1
where the time goes:
time: 1450 us; the launch traced here: 1440 us
  waiting for transfers between devices  993 us (68%)
  matrix products  235 us (16%)
  blocking collectives  100 us (7%)
  local copies, waits for them, and re-layouts  72.1 us (5%)
  other arithmetic  25.6 us (2%)
    all_gather x1, waiting for transfers between devices, body(): lax.all_gather(halves, 'col', axis=2, tiled=True)  986 us
    dot_general x8, matrix products, one(): jnp.einsum('arh,ahk->ark', piece, cauchy.astype(jnp.bfloat16), preferred_...  235 us
    all_gather x1, blocking collectives, body(): lax.all_gather(seam, ('col', 'depth'), axis=1, tiled=True)  68.2 us
  transfers between devices with their start and end apart: 2, of which 2 were waited for; matrix products, arithmetic and copies ran while one was open for 3% of the time, Pallas kernels for 0%

commit v1 on v0

--- a/solution.py
+++ b/solution.py
@@ -3,6 +3,11 @@
 import jax.numpy as jnp
 from jax import lax
 from jax.sharding import PartitionSpec as P
+
+
+def stack_and_merge(x, name, dim):
+    blocks = lax.all_gather(x, name)
+    return jnp.concatenate(blocks, axis=dim)
 
 
 def broadcast(shard, axis, root):
@@ -80,12 +85,7 @@
     ).reshape(2, ncols * shard_width)
     share = lower_col.shape[0] // ndepth
     product, sums = panel_product(
-        lax.all_gather(halves, "col", axis=2, tiled=True),
-        seam_mine,
-        value_mine,
-        lower_col,
-        width_col,
-        fraction,
+        stack_and_merge(halves, "col", 2), seam_mine, value_mine, lower_col, width_col, fraction
     )
     total = product
     product = lax.psum_scatter(total, "depth", scatter_dimension=2, tiled=True)

time: 1450 us -> 1490 us (1.028)
  local copies, waits for them, and re-layouts: 72.1 us -> 112 us
  blocking collectives: 100 us -> 127 us
  waiting for transfers between devices: 993 us -> 969 us
    reshape x0 -> x1, local copies, waits for them, and re-layouts: none -> 44.1 us  [stack_and_merge(): return jnp.concatenate(blocks, axis=dim)]
    all_gather x1, blocking collectives: 68.2 us -> 95.4 us  [body(): lax.all_gather(seam, ('col', 'depth'), axis=1, tiled=True)]
    all_gather x1, waiting for transfers between devices: 986 us -> 962 us  [stack_and_merge(): blocks = lax.all_gather(x, name)]
where the time goes in v1:
time: 1490 us
  waiting for transfers between devices  969 us (65%)
  matrix products  235 us (16%)
  blocking collectives  127 us (9%)
  local copies, waits for them, and re-layouts  112 us (8%)
  other arithmetic  25.7 us (2%)
    all_gather x1, waiting for transfers between devices, stack_and_merge(): blocks = lax.all_gather(x, name)  962 us
    dot_general x8, matrix products, one(): jnp.einsum('arh,ahk->ark', piece, cauchy.astype(jnp.bfloat16), preferred_...  235 us
    all_gather x1, blocking collectives, body(): lax.all_gather(seam, ('col', 'depth'), axis=1, tiled=True)  95.4 us
    reshape x1, local copies, waits for them, and re-layouts, stack_and_merge(): return jnp.concatenate(blocks, axis=dim)  44.1 us
  transfers between devices with their start and end apart: 2, of which 2 were waited for; matrix products, arithmetic and copies ran while one was open for 3% of the time, Pallas kernels for 0%

profile of v1, /device:TPU:0, one launch (start us, length us, event | category | flops | bytes accessed | tf_op | source)
XLA Modules:
  0.0 1488.1 jit_solution(8726411407510808642)
XLA Ops:
  6.5 0.7 all-gather.3.cloned.1.call-update
  7.3 15.7 %all_gather.13 = f32[2,16384]{1,0:T(2,128)S(1)} all-gather(f32[2,2048]{1,0:T(2,128)S(1)} %copy-done.4), channel_id=1, replica_groups=mesh['row'=4,'col'=4,'depth'=2] {'col','depth'}, dimensions={1}, use_global_device_ids=true | all-gather | bytes 147456 | tf_op jit(solution)/shard_map/all_gather | solution.py:74
  23.4 0.8 fusion.7
  24.2 16.1 %all-reduce = (bf16[1,2048]{1,0:T(2,128)(2,1)S(1)}, bf16[1,2048]{1,0:T(2,128)(2,1)S(1)}) all-reduce(bf16[1,2048]{1,0:T(2,128)(2,1)S(1)} %get-tuple-element.83, bf16[1,2048]{1,0:T(2,128)(2,1)S(1)} %get-tuple-element.82), channel_id=1, replica_groups=mesh['row'=4,'col'=4,'depth'=2] {'row'}, use_global_device_ids=true, to_apply=%region_1.0 | all-reduce | flops 4096 | bytes 16384 | tf_op jit(solution)/shard_map/psum | solution.py:15
  40.3 95.4 %all_gather.12 = f32[2,16384]{1,0:T(2,128)S(1)} all-gather(f32[2,2048]{1,0:T(2,128)S(1)} %maximum_convert_fusion), channel_id=1, replica_groups=mesh['row'=4,'col'=4,'depth'=2] {'col','depth'}, dimensions={1}, use_global_device_ids=true | all-gather | bytes 147456 | tf_op jit(solution)/shard_map/all_gather | solution.py:73
  136.7 4.9 copy.17
  141.6 6.9 reshape.81
  148.6 6.2 gather_fusion.1
  154.8 6.2 gather_fusion
  160.9 962.3 %all-gather.3.cloned.1.call-done = bf16[8,2048,2048]{2,1,0:T(8,128)(2,1)} async-done(((bf16[2,2048,2048]{2,1,0:T(8,128)(2,1)}), bf16[8,2048,2048]{2,1,0:T(8,128)(2,1)}) %all-gather.3.cloned.1.call-update) | async-done | bytes 67108880 | tf_op jit(solution)/shard_map/all_gather | solution.py:9
  1123.3 44.1 %copy.24 = bf16[4,2,256,8,2048]{4,3,0,2,1:T(8,128)(2,1)} copy(bf16[4,2,256,8,2048]{4,3,2,1,0:T(8,128)(2,1)} %bitcast.18) | data formatting | bytes 134217728 | tf_op jit(solution)/shard_map/reshape | solution.py:10
  1167.4 246.6 %while.10 = (s32[]{:T(128)}, f32[8,2,2048,128]{2,3,1,0:T(8,128)}, f32[2,4,2048]{2,1,0:T(4,128)S(1)}, f32[2,4,2048]{2,1,0:T(4,128)S(1)}, s32[8]{0:T(128)S(1)}, /*...) while((s32[]{:T(128)}, f32[8,2,2048,128]{2,3,1,0:T(8,128)}, ...), condition=%wide.region_3.5_spmd, body=%wide.region_2.4_spmd.sunk | while | flops 8598323200 | bytes 69603016 | solution.py:61
  1167.4 0.6 dynamic_slice.46
  1168.9 29.3 %fusion.17 = f32[8,2,2048,128]{2,3,1,0:T(8,128)} fusion(f32[8,2,2048,128]{2,3,1,0:T(8,128)} %get-tuple-element.175, s32[]{:T(128)S(6)} %copy.36, bf16[2,2048,8192]{2,1,0:T(8,128)(2,1)} %get-tuple-element.195, f32[128]{0:T(128)S(1)} %dynamic-slice_multiply_fusion.3, f32[128]{0:T(128)S(1)} %dynamic_slice.47, f32[2,8192]{1,0:T(2,128)S(1)} %bitcast.54, ...), kind=kOutput, calls=%fused_computation.9.clone.1 | convolution fusion | flops 8598323200 | bytes 69338112 | tf_op jit(solution)/shard_map/while/body/eval_jaxpr/arh,ahk->ark/dot_general | solution.py:56
  1198.2 0.6 dynamic_slice.46
  1199.7 29.3 %fusion.17 = f32[8,2,2048,128]{2,3,1,0:T(8,128)} fusion(f32[8,2,2048,128]{2,3,1,0:T(8,128)} %get-tuple-element.175, s32[]{:T(128)S(6)} %copy.36, bf16[2,2048,8192]{2,1,0:T(8,128)(2,1)} %get-tuple-element.195, f32[128]{0:T(128)S(1)} %dynamic-slice_multiply_fusion.3, f32[128]{0:T(128)S(1)} %dynamic_slice.47, f32[2,8192]{1,0:T(2,128)S(1)} %bitcast.54, ...), kind=kOutput, calls=%fused_computation.9.clone.1 | convolution fusion | flops 8598323200 | bytes 69338112 | tf_op jit(solution)/shard_map/while/body/eval_jaxpr/arh,ahk->ark/dot_general | solution.py:56
  1229.0 0.6 dynamic_slice.46
  1230.5 29.3 %fusion.17 = f32[8,2,2048,128]{2,3,1,0:T(8,128)} fusion(f32[8,2,2048,128]{2,3,1,0:T(8,128)} %get-tuple-element.175, s32[]{:T(128)S(6)} %copy.36, bf16[2,2048,8192]{2,1,0:T(8,128)(2,1)} %get-tuple-element.195, f32[128]{0:T(128)S(1)} %dynamic-slice_multiply_fusion.3, f32[128]{0:T(128)S(1)} %dynamic_slice.47, f32[2,8192]{1,0:T(2,128)S(1)} %bitcast.54, ...), kind=kOutput, calls=%fused_computation.9.clone.1 | convolution fusion | flops 8598323200 | bytes 69338112 | tf_op jit(solution)/shard_map/while/body/eval_jaxpr/arh,ahk->ark/dot_general | solution.py:56
  1259.8 0.6 dynamic_slice.46
  1261.3 29.3 %fusion.17 = f32[8,2,2048,128]{2,3,1,0:T(8,128)} fusion(f32[8,2,2048,128]{2,3,1,0:T(8,128)} %get-tuple-element.175, s32[]{:T(128)S(6)} %copy.36, bf16[2,2048,8192]{2,1,0:T(8,128)(2,1)} %get-tuple-element.195, f32[128]{0:T(128)S(1)} %dynamic-slice_multiply_fusion.3, f32[128]{0:T(128)S(1)} %dynamic_slice.47, f32[2,8192]{1,0:T(2,128)S(1)} %bitcast.54, ...), kind=kOutput, calls=%fused_computation.9.clone.1 | convolution fusion | flops 8598323200 | bytes 69338112 | tf_op jit(solution)/shard_map/while/body/eval_jaxpr/arh,ahk->ark/dot_general | solution.py:56
  1290.7 0.6 dynamic_slice.46
  1292.2 29.4 %fusion.17 = f32[8,2,2048,128]{2,3,1,0:T(8,128)} fusion(f32[8,2,2048,128]{2,3,1,0:T(8,128)} %get-tuple-element.175, s32[]{:T(128)S(6)} %copy.36, bf16[2,2048,8192]{2,1,0:T(8,128)(2,1)} %get-tuple-element.195, f32[128]{0:T(128)S(1)} %dynamic-slice_multiply_fusion.3, f32[128]{0:T(128)S(1)} %dynamic_slice.47, f32[2,8192]{1,0:T(2,128)S(1)} %bitcast.54, ...), kind=kOutput, calls=%fused_computation.9.clone.1 | convolution fusion | flops 8598323200 | bytes 69338112 | tf_op jit(solution)/shard_map/while/body/eval_jaxpr/arh,ahk->ark/dot_general | solution.py:56
  1321.5 0.6 dynamic_slice.46
  1323.0 29.3 %fusion.17 = f32[8,2,2048,128]{2,3,1,0:T(8,128)} fusion(f32[8,2,2048,128]{2,3,1,0:T(8,128)} %get-tuple-element.175, s32[]{:T(128)S(6)} %copy.36, bf16[2,2048,8192]{2,1,0:T(8,128)(2,1)} %get-tuple-element.195, f32[128]{0:T(128)S(1)} %dynamic-slice_multiply_fusion.3, f32[128]{0:T(128)S(1)} %dynamic_slice.47, f32[2,8192]{1,0:T(2,128)S(1)} %bitcast.54, ...), kind=kOutput, calls=%fused_computation.9.clone.1 | convolution fusion | flops 8598323200 | bytes 69338112 | tf_op jit(solution)/shard_map/while/body/eval_jaxpr/arh,ahk->ark/dot_general | solution.py:56
  1353.8 29.3 %fusion.17 = f32[8,2,2048,128]{2,3,1,0:T(8,128)} fusion(f32[8,2,2048,128]{2,3,1,0:T(8,128)} %get-tuple-element.175, s32[]{:T(128)S(6)} %copy.36, bf16[2,2048,8192]{2,1,0:T(8,128)(2,1)} %get-tuple-element.195, f32[128]{0:T(128)S(1)} %dynamic-slice_multiply_fusion.3, f32[128]{0:T(128)S(1)} %dynamic_slice.47, f32[2,8192]{1,0:T(2,128)S(1)} %bitcast.54, ...), kind=kOutput, calls=%fused_computation.9.clone.1 | convolution fusion | flops 8598323200 | bytes 69338112 | tf_op jit(solution)/shard_map/while/body/eval_jaxpr/arh,ahk->ark/dot_general | solution.py:56
  1384.7 29.3 %fusion.17 = f32[8,2,2048,128]{2,3,1,0:T(8,128)} fusion(f32[8,2,2048,128]{2,3,1,0:T(8,128)} %get-tuple-element.175, s32[]{:T(128)S(6)} %copy.36, bf16[2,2048,8192]{2,1,0:T(8,128)(2,1)} %get-tuple-element.195, f32[128]{0:T(128)S(1)} %dynamic-slice_multiply_fusion.3, f32[128]{0:T(128)S(1)} %dynamic_slice.47, f32[2,8192]{1,0:T(2,128)S(1)} %bitcast.54, ...), kind=kOutput, calls=%fused_computation.9.clone.1 | convolution fusion | flops 8598323200 | bytes 69338112 | tf_op jit(solution)/shard_map/while/body/eval_jaxpr/arh,ahk->ark/dot_general | solution.py:56
  1414.0 18.1 %copy.19 = f32[2,2048,8,128]{3,2,1,0:T(8,128)} copy(f32[2,2048,8,128]{1,3,0,2:T(8,128)} %bitcast.48) | data formatting | bytes 33554432 | tf_op jit(solution)/shard_map/transpose | solution.py:62
  1432.1 18.0 %reshape.84 = f32[2,2048,1024]{2,1,0:T(8,128)} reshape(f32[2,2048,8,128]{3,2,1,0:T(8,128)} %copy.19) | data formatting | bytes 33554432 | tf_op jit(solution)/shard_map/reshape | solution.py:62
  1450.3 0.7 copy-done.3
  1451.1 16.1 %multiply_reduce_fusion.6 = (f32[512]{0:T(512)S(1)}, f32[512]{0:T(512)S(1)}, f32[512]{0:T(512)S(1)}, f32[512]{0:T(512)S(1)}, f32[512]{0:T(512)S(1)}, /*index=5*/f32[512]{0:T(512)S(1)}, f32[512]{0:T(512)S(1)}, f32[512]{0:T(512)S(1)}) fusion(f32[2,2048]{1,0:T(2,128)S(1)} %get-tuple-element.99, f32[2,2048]{1,0:T(2,128)S(1)} %get-tuple-element.91, ...), kind=kLoop, calls=%fused_computation.17 | loop fusion | flops 83881984 | bytes 282624 | tf_op jit(solution)/shard_map/reduce_sum | solution.py:42
  1467.3 6.2 reduce-scatter.2.cloned.1.call-done
  1473.4 7.9 broadcast_divide_fusion
  (68 shorter events, 4.8 us)
Async XLA Ops:
  6.5 0.8 copy-start.4
  6.5 1116.7 %all-gather.3.cloned.1.call-start = ((), (), s32[]{:S(2)}) async-start(), calls=%async_computation.2 | async-start | bytes 83886080 | tf_op jit(solution)/shard_map/all_gather | solution.py:9
  7.3 1466.2 %reduce-scatter.2.cloned.1.call-start = ((), (), s32[]{:S(2)}) async-start(), calls=%async_computation.1 | async-start | bytes 25165824 | tf_op jit(solution)/shard_map/reduce_scatter | solution.py:91
  23.1 113.6 %copy-start = (f32[2,16384]{1,0:T(2,128)}, f32[2,16384]{1,0:T(2,128)S(1)}, u32[]{:S(2)}) copy-start(f32[2,16384]{1,0:T(2,128)S(1)} %all_gather.13) | copy-start | bytes 393220
  135.7 0.7 copy-start.2
  136.7 11.9 copy-start.5
  1123.3 44.1 %copy-start.6 = (f32[1024]{0:T(1024)S(1)}, f32[1024]{0:T(1024)}, u32[]{:S(2)}) copy-start(f32[1024]{0:T(1024)} %param.11) | copy-start | bytes 12292
  1450.1 0.9 copy-start.3
  1450.2 1.0 copy-start.1
Sparse Core Ops, SparseCore 0:
  8.9 1114.3 all-gather.2
  1450.3 23.0 reduce-scatter.1
